TPU v7x, 32 devices: a whole 2x2x4 slice. The times are simulated.
32 devices in a mesh: zero: 16 (over z, x, core), tensor: 2 (over y).
Axes of the slice: x: 2, y: 2, z: 4, core: 2. Of those that a mesh axis runs over, the one named last changes fastest.
Arguments:
- grads: bfloat16 [16, 2, 16, 49152], P('zero', None, None, 'tensor'), may hold values from -1200 to 1200
- moment1: bfloat16 [2, 16, 49152], P(None, 'zero', 'tensor'), may hold values from -1 to 1
- moment2: float32 [2, 16, 49152], P(None, 'zero', 'tensor'), may hold values from 0.01 to 0.2
- master: float32 [2, 16, 49152], P(None, 'zero', 'tensor'), may hold values from -0.008 to 0.008
Outputs:
- new_moment1: bfloat16 [2, 16, 49152], P(None, 'zero', 'tensor')
- new_moment2: float32 [2, 16, 49152], P(None, 'zero', 'tensor')
- new_master: float32 [2, 16, 49152], P(None, 'zero', 'tensor')
- weights: bfloat16 [2, 16, 49152], P(None, None, 'tensor')
All inputs are finite; a program needn't handle non-finite values. Where the computation divides by a largest or mean magnitude, that divisor is 1e-20 or more.
Results may differ from a plain program's by a relative error of at most 0.0053.
Values may be sent and summed in bfloat16 or wider, within the bound.
A program may use at most 64 MiB of HBM per device.

v0:
```python
import jax
import jax.numpy as jnp
from jax import lax
from jax.sharding import PartitionSpec as P

decay_first = 0.9
decay_second = 0.95
learn_rate = 0.001
weight_decay = 0.1
adam_epsilon = 1e-08
peak_epsilon = 1e-06
bias_first = 1.0 - 0.9**10
bias_second = 1.0 - 0.95**10


def update_rows(gsum, moment1, moment2, master):
    new_moment1 = (decay_first * moment1.astype(jnp.float32) + (1.0 - decay_first) * gsum).astype(
        jnp.bfloat16
    )
    new_moment2 = decay_second * moment2 + (1.0 - decay_second) * gsum * gsum
    stored = lax.optimization_barrier(new_moment1).astype(jnp.float32)
    step_dir = stored / bias_first / (jnp.sqrt(new_moment2 / bias_second) + adam_epsilon)
    new_master = master - learn_rate * (step_dir + weight_decay * master)
    local_peak = jnp.max(jnp.abs(new_master), axis=(1, 2))
    wpeak = lax.pmax(local_peak, ("zero", "tensor")) + peak_epsilon
    normed = (new_master / wpeak[:, None, None]).astype(jnp.bfloat16)
    weights = lax.all_gather(normed, "zero", axis=1, tiled=True)
    return (new_moment1, new_moment2, new_master, weights)


def local(grads, moment1, moment2, master):
    local_peak = jnp.max(jnp.abs(grads), axis=(0, 2, 3)).astype(jnp.float32)
    peak = lax.pmax(local_peak, ("zero", "tensor")) + peak_epsilon
    scaled_half = (grads.astype(jnp.float32) / peak[None, :, None, None]).astype(jnp.bfloat16)
    received = lax.all_to_all(scaled_half, "zero", split_axis=2, concat_axis=0, tiled=True)
    gsum = jnp.sum(received.astype(jnp.float32), axis=0)
    return update_rows(gsum, moment1, moment2, master)


def solution(mesh):
    placed = (
        P("zero", None, None, "tensor"),
        P(None, "zero", "tensor"),
        P(None, "zero", "tensor"),
        P(None, "zero", "tensor"),
    )
    return jax.shard_map(
        local,
        mesh=mesh,
        in_specs=placed,
        out_specs=(
            P(None, "zero", "tensor"),
            P(None, "zero", "tensor"),
            P(None, "zero", "tensor"),
            P(None, None, "tensor"),
        ),
        check_vma=False,
    )
```

profile of v0, /device:TPU:0, one launch (start us, length us, event | category | flops | bytes accessed | tf_op | source)
XLA Modules:
  0.0 187.2 jit_solution(13088254821506365265)
XLA Ops:
  7.2 0.0 copy-start
  7.2 0.0 all-gather.2.cloned.1.call-start
  7.2 1.8 abs_reduce_fusion
  9.0 42.0 %pmax.14 = f32[2]{0:T(128)S(1)} all-reduce(bf16[2]{0:T(256)(128)(2,1)S(1)} %abs_reduce_fusion), channel_id=1, replica_groups=mesh['zero'=16,'tensor'=2] {'zero','tensor'}, use_global_device_ids=true, to_apply=%region_1.0 | all-reduce | flops 2 | bytes 12 | tf_op jit(solution)/shard_map/pmax | solution.py:33
  51.0 0.0 copy-done
  51.0 0.3 divide_convert_fusion
  51.3 1.6 copy.17
  52.9 41.1 %all_to_all.4 = bf16[1,2,16,24576]{3,1,0,2:T(2,128)(2,1)S(1)} all-to-all(bf16[1,2,16,24576]{3,1,0,2:T(2,128)(2,1)S(1)} %copy.17), channel_id=1, replica_groups=mesh['zero'=16,'tensor'=2] {'zero'}, dimensions={2} | all-to-all | bytes 3145728 | tf_op jit(solution)/shard_map/all_to_all | solution.py:35
  94.1 0.0 copy-start.4
  94.1 0.0 copy-start.2
  94.1 0.0 copy-start.3
  94.1 1.4 convert_reduce_fusion
  95.4 0.0 copy-done.4
  95.4 0.2 fusion.2
  95.6 0.0 copy-done.2
  95.6 0.0 copy-done.3
  95.6 0.0 copy-start.1
  95.6 0.8 abs_reduce_fusion.1
  96.5 40.1 %pmax.15 = f32[2]{0:T(128)S(1)} all-reduce(f32[2]{0:T(128)S(1)} %get-tuple-element.16), channel_id=1, replica_groups=mesh['zero'=16,'tensor'=2] {'zero','tensor'}, use_global_device_ids=true, to_apply=%region_4.0 | all-reduce | flops 2 | bytes 16 | tf_op jit(solution)/shard_map/pmax | solution.py:25
  136.6 0.8 divide_convert_fusion.1
  137.4 0.0 all-gather.2.cloned.1.call-update
  137.4 0.9 copy.22
  138.3 0.9 copy.21
  139.2 37.7 %all-gather.2.cloned.1.call-done = bf16[2,16,24576]{2,0,1:T(2,128)(2,1)} async-done(((bf16[2,1,24576]{2,0,1:T(2,128)(2,1)}), bf16[2,16,24576]{2,0,1:T(2,128)(2,1)}) %all-gather.2.cloned.1.call-update) | async-done | bytes 1572880 | tf_op jit(solution)/shard_map/all_gather | solution.py:27
  176.9 3.4 %copy.23 = bf16[2,16,24576]{2,1,0:T(8,128)(2,1)} copy(bf16[2,16,24576]{2,0,1:T(2,128)(2,1)} %all-gather.2.cloned.1.call-done) | data formatting | bytes 3145728
  180.3 0.0 copy-done.1
  (2 shorter events, 0.0 us)
Async XLA Ops:
  7.2 43.8 %copy-start = (bf16[1,2,16,24576]{3,2,1,0:T(8,128)(2,1)S(1)}, bf16[1,2,16,24576]{3,2,1,0:T(8,128)(2,1)}, u32[]{:S(2)}) copy-start(bf16[1,2,16,24576]{3,2,1,0:T(8,128)(2,1)} %param.4) | copy-start | bytes 4718596
  7.2 169.7 %all-gather.2.cloned.1.call-start = ((), (), s32[]{:S(2)}) async-start(), calls=%async_computation.1 | async-start | bytes 1671168 | tf_op jit(solution)/shard_map/all_gather | solution.py:27
  94.1 1.4 copy-start.4
  94.1 1.6 copy-start.2
  94.1 1.6 copy-start.3
  95.6 84.7 %copy-start.1 = (bf16[2,1,24576]{2,0,1:T(2,128)(2,1)}, bf16[2,1,24576]{2,0,1:T(2,128)(2,1)S(1)}, u32[]{:S(2)}) copy-start(bf16[2,1,24576]{2,0,1:T(2,128)(2,1)S(1)} %fusion.2) | copy-start | bytes 294916
Sparse Core Ops, SparseCore 0:
  137.5 39.3 all-gather.1
where the time goes:
time: 188 us; the launch traced here: 187 us
  blocking collectives  123 us (65%)
  waiting for transfers between devices  37.8 us (20%)
  between operations  14.1 us (8%)
  local copies, waits for them, and re-layouts  6.81 us (4%)
  other arithmetic  5.24 us (3%)
    pmax x1, blocking collectives, local(): peak = lax.pmax(local_peak, ('zero', 'tensor')) + peak_epsilon  42 us
    all_to_all x1, blocking collectives, local(): lax.all_to_all(scaled_half, 'zero', split_axis=2, concat_axis=0, tiled=True)  41.1 us
    pmax x1, blocking collectives, update_rows(): wpeak = lax.pmax(local_peak, ('zero', 'tensor')) + peak_epsilon  40.1 us
    all_gather x1, waiting for transfers between devices, update_rows(): weights = lax.all_gather(normed, 'zero', axis=1, tiled=True)  37.7 us
    unnamed x13, local copies, waits for them, and re-layouts  5.2 us
  transfers between devices with their start and end apart: 1, of which 1 were waited for; matrix products, arithmetic and copies ran while one was open for 1% of the time, Pallas kernels for 0%

commit v1 on v0

--- a/solution.py
+++ b/solution.py
@@ -13,6 +13,31 @@
 bias_second = 1.0 - 0.95**10
 
 
+def detail_knots(z_in):
+    carry_in, value_now, carry_out = (lax.axis_size("zero"), lax.axis_index("zero"), z_in.shape[1])
+    rows = []
+    for src_i in range(carry_in):
+        rows.append((src_i, (src_i + 1) % carry_in))
+    leaves = []
+    for src_i in range(carry_in):
+        leaves.append((src_i, (src_i - 1) % carry_in))
+    before = jnp.zeros((*z_in.shape[:1], carry_in * carry_out, *z_in.shape[2:]), z_in.dtype)
+    before = lax.dynamic_update_slice_in_dim(before, z_in, value_now * carry_out, axis=1)
+    v_now = w1 = z_in
+    side_arr = carry_in // 2
+    for b in range(1, side_arr + 1):
+        v_now = lax.ppermute(v_now, "zero", rows)
+        before = lax.dynamic_update_slice_in_dim(
+            before, v_now, (value_now - b) % carry_in * carry_out, axis=1
+        )
+        if b < carry_in - side_arr:
+            w1 = lax.ppermute(w1, "zero", leaves)
+            before = lax.dynamic_update_slice_in_dim(
+                before, w1, (value_now + b) % carry_in * carry_out, axis=1
+            )
+    return before
+
+
 def update_rows(gsum, moment1, moment2, master):
     new_moment1 = (decay_first * moment1.astype(jnp.float32) + (1.0 - decay_first) * gsum).astype(
         jnp.bfloat16
@@ -24,7 +49,7 @@
     local_peak = jnp.max(jnp.abs(new_master), axis=(1, 2))
     wpeak = lax.pmax(local_peak, ("zero", "tensor")) + peak_epsilon
     normed = (new_master / wpeak[:, None, None]).astype(jnp.bfloat16)
-    weights = lax.all_gather(normed, "zero", axis=1, tiled=True)
+    weights = detail_knots(normed)
     return (new_moment1, new_moment2, new_master, weights)
 
 

time: 188 us -> 238 us (1.27)
  local copies, waits for them, and re-layouts: 6.81 us -> 60.9 us
  starting transfers between devices: 0.04 us -> 31.7 us
  waiting for transfers between devices: 37.8 us -> 15.7 us
  between operations: 14.1 us -> 1.01 us
    dynamic_update_slice x0 -> x16, local copies, waits for them, and re-layouts: none -> 53.8 us  [the longest x8 26.9 us: detail_knots(): lax.dynamic_update_slice_in_dim(before, v_now, (value_now - b) % carry_in...]
    all_gather x1 -> x0, waiting for transfers between devices: 37.7 us -> none  [update_rows(): weights = lax.all_gather(normed, 'zero', axis=1, tiled=True)]
    ppermute x0 -> x15, starting transfers between devices: none -> 31.7 us  [the longest x7 31.6 us: detail_knots(): w1 = lax.ppermute(w1, 'zero', leaves)]
    ppermute x0 -> x15, waiting for transfers between devices: none -> 15.7 us  [the longest x8 15.6 us: detail_knots(): v_now = lax.ppermute(v_now, 'zero', rows)]
    unnamed x13 -> x14, local copies, waits for them, and re-layouts: 5.2 us -> 2.92 us
  transfers between devices with their start and end apart: 1 -> 15, of which waited for: 1 -> 8; matrix products, arithmetic and copies ran while one was open for 1% -> 23% of each run, Pallas kernels for 0% -> 0%
where the time goes in v1:
time: 238 us; the launch traced here: 237 us
  blocking collectives  123 us (52%)
  local copies, waits for them, and re-layouts  60.9 us (26%)
  starting transfers between devices  31.7 us (13%)
  waiting for transfers between devices  15.7 us (7%)
  other arithmetic  4.61 us (2%)
    pmax x1, blocking collectives, local(): peak = lax.pmax(local_peak, ('zero', 'tensor')) + peak_epsilon  42 us
    all_to_all x1, blocking collectives, local(): lax.all_to_all(scaled_half, 'zero', split_axis=2, concat_axis=0, tiled=True)  41.1 us
    pmax x1, blocking collectives, update_rows(): wpeak = lax.pmax(local_peak, ('zero', 'tensor')) + peak_epsilon  40.1 us
    ppermute x7, starting transfers between devices, detail_knots(): w1 = lax.ppermute(w1, 'zero', leaves)  31.6 us
    dynamic_update_slice x8, local copies, waits for them, and re-layouts, detail_knots(): lax.dynamic_update_slice_in_dim(before, v_now, (value_now - b) % carry_in...  26.9 us
    dynamic_update_slice x7, local copies, waits for them, and re-layouts, detail_knots(): lax.dynamic_update_slice_in_dim(before, w1, (value_now + b) % carry_in *...  23.5 us
    ppermute x8, waiting for transfers between devices, detail_knots(): v_now = lax.ppermute(v_now, 'zero', rows)  15.6 us
  transfers between devices with their start and end apart: 15, of which 8 were waited for; matrix products, arithmetic and copies ran while one was open for 23% of the time, Pallas kernels for 0%

profile of v1, /device:TPU:0, one launch (start us, length us, event | category | flops | bytes accessed | tf_op | source)
XLA Modules:
  0.0 237.1 jit_solution(6466603162862122773)
XLA Ops:
  0.6 1.8 abs_reduce_fusion
  2.4 42.0 %pmax.14 = f32[2]{0:T(128)S(1)} all-reduce(bf16[2]{0:T(256)(128)(2,1)S(1)} %abs_reduce_fusion), channel_id=1, replica_groups=mesh['zero'=16,'tensor'=2] {'zero','tensor'}, use_global_device_ids=true, to_apply=%region_1.0 | all-reduce | flops 2 | bytes 12 | tf_op jit(solution)/shard_map/pmax | solution.py:58
  44.4 0.3 divide_convert_fusion
  44.7 1.6 copy.32
  46.3 41.1 %all_to_all.4 = bf16[1,2,16,24576]{3,1,0,2:T(2,128)(2,1)S(1)} all-to-all(bf16[1,2,16,24576]{3,1,0,2:T(2,128)(2,1)S(1)} %copy.32), channel_id=1, replica_groups=mesh['zero'=16,'tensor'=2] {'zero'}, dimensions={2} | all-to-all | bytes 3145728 | tf_op jit(solution)/shard_map/all_to_all | solution.py:60
  87.5 1.4 convert_reduce_fusion
  88.8 0.2 fusion.2
  89.0 0.0 copy-start.2
  89.1 0.8 abs_reduce_fusion.1
  89.9 40.1 %pmax.15 = f32[2]{0:T(128)S(1)} all-reduce(f32[2]{0:T(128)S(1)} %get-tuple-element.16), channel_id=1, replica_groups=mesh['zero'=16,'tensor'=2] {'zero','tensor'}, use_global_device_ids=true, to_apply=%region_4.0 | all-reduce | flops 2 | bytes 16 | tf_op jit(solution)/shard_map/pmax | solution.py:50
  130.0 0.1 divide_convert_fusion.1
  130.1 0.1 collective-permute-start
  130.2 4.4 %collective-permute-start.1 = (bf16[2,1,24576]{2,0,1:T(2,128)(2,1)S(1)}, bf16[2,1,24576]{2,0,1:T(2,128)(2,1)S(1)}, u32[]{:S(2)}, u32[]{:S(2)}) collective-permute-start(bf16[2,1,24576]{2,0,1:T(2,128)(2,1)S(1)} %divide_convert_fusion.1), channel_id=1, source_target_pairs={{0,30},{2,0},{4,2},{6,4},{8,6},{10,8},{12,10},{14,12},{16,14},{18,... | collective-permute-start | bytes 294920 | tf_op jit(solution)/shard_map/ppermute | solution.py:34
  134.6 2.4 %collective-permute-done = bf16[2,1,24576]{2,0,1:T(2,128)(2,1)S(1)} collective-permute-done((bf16[2,1,24576]{2,0,1:T(2,128)(2,1)S(1)}, bf16[2,1,24576]{2,0,1:T(2,128)(2,1)S(1)}, u32[]{:S(2)}, u32[]{:S(2)}) %collective-permute-start) | collective-permute-done | bytes 98336 | tf_op jit(solution)/shard_map/ppermute | solution.py:29
  137.0 4.4 %collective-permute-start.3 = (bf16[2,1,24576]{2,0,1:T(2,128)(2,1)S(1)}, bf16[2,1,24576]{2,0,1:T(2,128)(2,1)S(1)}, u32[]{:S(2)}, u32[]{:S(2)}) collective-permute-start(bf16[2,1,24576]{2,0,1:T(2,128)(2,1)S(1)} %collective-permute-done.1), channel_id=1, source_target_pairs={{0,30},{2,0},{4,2},{6,4},{8,6},{10,8},{12,10},{14,12},{16,14},{18,... | collective-permute-start | bytes 294920 | tf_op jit(solution)/shard_map/ppermute | solution.py:34
  141.5 2.3 collective-permute-done.2
  143.8 4.4 %collective-permute-start.5 = (bf16[2,1,24576]{2,0,1:T(2,128)(2,1)S(1)}, bf16[2,1,24576]{2,0,1:T(2,128)(2,1)S(1)}, u32[]{:S(2)}, u32[]{:S(2)}) collective-permute-start(bf16[2,1,24576]{2,0,1:T(2,128)(2,1)S(1)} %collective-permute-done.3), channel_id=1, source_target_pairs={{0,30},{2,0},{4,2},{6,4},{8,6},{10,8},{12,10},{14,12},{16,14},{18,... | collective-permute-start | bytes 294920 | tf_op jit(solution)/shard_map/ppermute | solution.py:34
  148.2 2.3 collective-permute-done.4
  150.5 4.5 %collective-permute-start.7 = (bf16[2,1,24576]{2,0,1:T(2,128)(2,1)S(1)}, bf16[2,1,24576]{2,0,1:T(2,128)(2,1)S(1)}, u32[]{:S(2)}, u32[]{:S(2)}) collective-permute-start(bf16[2,1,24576]{2,0,1:T(2,128)(2,1)S(1)} %collective-permute-done.5), channel_id=1, source_target_pairs={{0,30},{2,0},{4,2},{6,4},{8,6},{10,8},{12,10},{14,12},{16,14},{18,... | collective-permute-start | bytes 294920 | tf_op jit(solution)/shard_map/ppermute | solution.py:34
  155.1 2.3 collective-permute-done.6
  157.4 4.5 %collective-permute-start.9 = (bf16[2,1,24576]{2,0,1:T(2,128)(2,1)S(1)}, bf16[2,1,24576]{2,0,1:T(2,128)(2,1)S(1)}, u32[]{:S(2)}, u32[]{:S(2)}) collective-permute-start(bf16[2,1,24576]{2,0,1:T(2,128)(2,1)S(1)} %collective-permute-done.7), channel_id=1, source_target_pairs={{0,30},{2,0},{4,2},{6,4},{8,6},{10,8},{12,10},{14,12},{16,14},{18,... | collective-permute-start | bytes 294920 | tf_op jit(solution)/shard_map/ppermute | solution.py:34
  161.9 2.2 collective-permute-done.8
  164.1 0.0 collective-permute-done.9
  164.1 4.6 %collective-permute-start.11 = (bf16[2,1,24576]{2,0,1:T(2,128)(2,1)S(1)}, bf16[2,1,24576]{2,0,1:T(2,128)(2,1)S(1)}, u32[]{:S(2)}, u32[]{:S(2)}) collective-permute-start(bf16[2,1,24576]{2,0,1:T(2,128)(2,1)S(1)} %collective-permute-done.9), channel_id=1, source_target_pairs={{0,30},{2,0},{4,2},{6,4},{8,6},{10,8},{12,10},{14,12},{16,14},{18,... | collective-permute-start | bytes 294920 | tf_op jit(solution)/shard_map/ppermute | solution.py:34
  168.7 2.1 collective-permute-done.10
  170.8 0.1 collective-permute-done.11
  171.0 4.6 %collective-permute-start.13 = (bf16[2,1,24576]{2,0,1:T(2,128)(2,1)S(1)}, bf16[2,1,24576]{2,0,1:T(2,128)(2,1)S(1)}, u32[]{:S(2)}, u32[]{:S(2)}) collective-permute-start(bf16[2,1,24576]{2,0,1:T(2,128)(2,1)S(1)} %collective-permute-done.11), channel_id=1, source_target_pairs={{0,30},{2,0},{4,2},{6,4},{8,6},{10,8},{12,10},{14,12},{16,14},{18,... | collective-permute-start | bytes 294920 | tf_op jit(solution)/shard_map/ppermute | solution.py:34
  175.6 2.0 collective-permute-done.12
  177.6 0.9 copy.53
  178.5 0.2 copy.36
  178.6 0.9 copy.52
  179.5 0.1 broadcast_in_dim.2
  179.6 3.4 %dynamic_update_slice.48 = bf16[2,16,24576]{2,1,0:T(8,128)(2,1)S(1)} dynamic-update-slice(bf16[2,16,24576]{2,1,0:T(8,128)(2,1)S(1)} %broadcast_in_dim.2, bf16[2,1,24576]{2,1,0:T(2,128)(2,1)S(1)} %copy.36, s32[]{:T(128)} %constant.115.clone.1, s32[]{:T(128)S(6)} %select_n.111, s32[]{:T(128)} %constant.115.clone.1) | dynamic-update-slice | bytes 196612 | tf_op jit(solution)/shard_map/dynamic_update_slice | solution.py:25
  183.0 0.2 copy.37
  183.2 3.4 %dynamic_update_slice.49 = bf16[2,16,24576]{2,1,0:T(8,128)(2,1)S(1)} dynamic-update-slice(bf16[2,16,24576]{2,1,0:T(8,128)(2,1)S(1)} %dynamic_update_slice.48, bf16[2,1,24576]{2,1,0:T(2,128)(2,1)S(1)} %copy.37, s32[]{:T(128)} %constant.115.clone.1, s32[]{:T(128)S(6)} %select_n.113, s32[]{:T(128)} %constant.115.clone.1) | dynamic-update-slice | bytes 196612 | tf_op jit(solution)/shard_map/dynamic_update_slice | solution.py:30
  186.5 0.2 copy.38
  186.7 3.4 %dynamic_update_slice.50 = bf16[2,16,24576]{2,1,0:T(8,128)(2,1)S(1)} dynamic-update-slice(bf16[2,16,24576]{2,1,0:T(8,128)(2,1)S(1)} %dynamic_update_slice.49, bf16[2,1,24576]{2,1,0:T(2,128)(2,1)S(1)} %copy.38, s32[]{:T(128)} %constant.115.clone.1, s32[]{:T(128)S(6)} %select_n.115, s32[]{:T(128)} %constant.115.clone.1) | dynamic-update-slice | bytes 196612 | tf_op jit(solution)/shard_map/dynamic_update_slice | solution.py:35
  190.1 0.2 copy.39
  190.2 3.4 %dynamic_update_slice.51 = bf16[2,16,24576]{2,1,0:T(8,128)(2,1)S(1)} dynamic-update-slice(bf16[2,16,24576]{2,1,0:T(8,128)(2,1)S(1)} %dynamic_update_slice.50, bf16[2,1,24576]{2,1,0:T(2,128)(2,1)S(1)} %copy.39, s32[]{:T(128)} %constant.115.clone.1, s32[]{:T(128)S(6)} %select_n.117, s32[]{:T(128)} %constant.115.clone.1) | dynamic-update-slice | bytes 196612 | tf_op jit(solution)/shard_map/dynamic_update_slice | solution.py:30
  193.6 0.2 copy.40
  193.7 3.4 %dynamic_update_slice.52 = bf16[2,16,24576]{2,1,0:T(8,128)(2,1)S(1)} dynamic-update-slice(bf16[2,16,24576]{2,1,0:T(8,128)(2,1)S(1)} %dynamic_update_slice.51, bf16[2,1,24576]{2,1,0:T(2,128)(2,1)S(1)} %copy.40, s32[]{:T(128)} %constant.115.clone.1, s32[]{:T(128)S(6)} %select_n.119, s32[]{:T(128)} %constant.115.clone.1) | dynamic-update-slice | bytes 196612 | tf_op jit(solution)/shard_map/dynamic_update_slice | solution.py:35
  197.1 0.2 copy.41
  197.3 3.4 %dynamic_update_slice.53 = bf16[2,16,24576]{2,1,0:T(8,128)(2,1)S(1)} dynamic-update-slice(bf16[2,16,24576]{2,1,0:T(8,128)(2,1)S(1)} %dynamic_update_slice.52, bf16[2,1,24576]{2,1,0:T(2,128)(2,1)S(1)} %copy.41, s32[]{:T(128)} %constant.115.clone.1, s32[]{:T(128)S(6)} %select_n.121, s32[]{:T(128)} %constant.115.clone.1) | dynamic-update-slice | bytes 196612 | tf_op jit(solution)/shard_map/dynamic_update_slice | solution.py:30
  200.6 0.2 copy.42
  200.8 3.4 %dynamic_update_slice.54 = bf16[2,16,24576]{2,1,0:T(8,128)(2,1)S(1)} dynamic-update-slice(bf16[2,16,24576]{2,1,0:T(8,128)(2,1)S(1)} %dynamic_update_slice.53, bf16[2,1,24576]{2,1,0:T(2,128)(2,1)S(1)} %copy.42, s32[]{:T(128)} %constant.115.clone.1, s32[]{:T(128)S(6)} %select_n.123, s32[]{:T(128)} %constant.115.clone.1) | dynamic-update-slice | bytes 196612 | tf_op jit(solution)/shard_map/dynamic_update_slice | solution.py:35
  204.2 0.2 copy.43
  204.3 3.4 %dynamic_update_slice.55 = bf16[2,16,24576]{2,1,0:T(8,128)(2,1)S(1)} dynamic-update-slice(bf16[2,16,24576]{2,1,0:T(8,128)(2,1)S(1)} %dynamic_update_slice.54, bf16[2,1,24576]{2,1,0:T(2,128)(2,1)S(1)} %copy.43, s32[]{:T(128)} %constant.115.clone.1, s32[]{:T(128)S(6)} %select_n.125, s32[]{:T(128)} %constant.115.clone.1) | dynamic-update-slice | bytes 196612 | tf_op jit(solution)/shard_map/dynamic_update_slice | solution.py:30
  207.7 0.2 copy.44
  207.9 3.4 %dynamic_update_slice.56 = bf16[2,16,24576]{2,1,0:T(8,128)(2,1)S(1)} dynamic-update-slice(bf16[2,16,24576]{2,1,0:T(8,128)(2,1)S(1)} %dynamic_update_slice.55, bf16[2,1,24576]{2,1,0:T(2,128)(2,1)S(1)} %copy.44, s32[]{:T(128)} %constant.115.clone.1, s32[]{:T(128)S(6)} %select_n.127, s32[]{:T(128)} %constant.115.clone.1) | dynamic-update-slice | bytes 196612 | tf_op jit(solution)/shard_map/dynamic_update_slice | solution.py:35
  211.2 0.2 copy.45
  211.4 3.4 %dynamic_update_slice.57 = bf16[2,16,24576]{2,1,0:T(8,128)(2,1)S(1)} dynamic-update-slice(bf16[2,16,24576]{2,1,0:T(8,128)(2,1)S(1)} %dynamic_update_slice.56, bf16[2,1,24576]{2,1,0:T(2,128)(2,1)S(1)} %copy.45, s32[]{:T(128)} %constant.115.clone.1, s32[]{:T(128)S(6)} %select_n.129, s32[]{:T(128)} %constant.115.clone.1) | dynamic-update-slice | bytes 196612 | tf_op jit(solution)/shard_map/dynamic_update_slice | solution.py:30
  214.8 0.2 copy.46
  214.9 3.4 %dynamic_update_slice.58 = bf16[2,16,24576]{2,1,0:T(8,128)(2,1)S(1)} dynamic-update-slice(bf16[2,16,24576]{2,1,0:T(8,128)(2,1)S(1)} %dynamic_update_slice.57, bf16[2,1,24576]{2,1,0:T(2,128)(2,1)S(1)} %copy.46, s32[]{:T(128)} %constant.115.clone.1, s32[]{:T(128)S(6)} %select_n.131, s32[]{:T(128)} %constant.115.clone.1) | dynamic-update-slice | bytes 196612 | tf_op jit(solution)/shard_map/dynamic_update_slice | solution.py:35
  218.3 0.2 copy.47
  218.5 3.4 %dynamic_update_slice.59 = bf16[2,16,24576]{2,1,0:T(8,128)(2,1)S(1)} dynamic-update-slice(bf16[2,16,24576]{2,1,0:T(8,128)(2,1)S(1)} %dynamic_update_slice.58, bf16[2,1,24576]{2,1,0:T(2,128)(2,1)S(1)} %copy.47, s32[]{:T(128)} %constant.115.clone.1, s32[]{:T(128)S(6)} %select_n.133, s32[]{:T(128)} %constant.115.clone.1) | dynamic-update-slice | bytes 196612 | tf_op jit(solution)/shard_map/dynamic_update_slice | solution.py:30
  221.8 0.2 copy.48
  222.0 3.4 %dynamic_update_slice.60 = bf16[2,16,24576]{2,1,0:T(8,128)(2,1)S(1)} dynamic-update-slice(bf16[2,16,24576]{2,1,0:T(8,128)(2,1)S(1)} %dynamic_update_slice.59, bf16[2,1,24576]{2,1,0:T(2,128)(2,1)S(1)} %copy.48, s32[]{:T(128)} %constant.115.clone.1, s32[]{:T(128)S(6)} %select_n.135, s32[]{:T(128)} %constant.115.clone.1) | dynamic-update-slice | bytes 196612 | tf_op jit(solution)/shard_map/dynamic_update_slice | solution.py:35
  225.4 0.2 copy.49
  225.5 3.4 %dynamic_update_slice.61 = bf16[2,16,24576]{2,1,0:T(8,128)(2,1)S(1)} dynamic-update-slice(bf16[2,16,24576]{2,1,0:T(8,128)(2,1)S(1)} %dynamic_update_slice.60, bf16[2,1,24576]{2,1,0:T(2,128)(2,1)S(1)} %copy.49, s32[]{:T(128)} %constant.115.clone.1, s32[]{:T(128)S(6)} %select_n.137, s32[]{:T(128)} %constant.115.clone.1) | dynamic-update-slice | bytes 196612 | tf_op jit(solution)/shard_map/dynamic_update_slice | solution.py:30
  228.9 0.2 copy.50
  229.1 3.4 %dynamic_update_slice.62 = bf16[2,16,24576]{2,1,0:T(8,128)(2,1)S(1)} dynamic-update-slice(bf16[2,16,24576]{2,1,0:T(8,128)(2,1)S(1)} %dynamic_update_slice.61, bf16[2,1,24576]{2,1,0:T(2,128)(2,1)S(1)} %copy.50, s32[]{:T(128)} %constant.115.clone.1, s32[]{:T(128)S(6)} %select_n.139, s32[]{:T(128)} %constant.115.clone.1) | dynamic-update-slice | bytes 196612 | tf_op jit(solution)/shard_map/dynamic_update_slice | solution.py:35
  232.4 0.2 copy.51
  232.6 3.4 %dynamic_update_slice.63 = bf16[2,16,24576]{2,1,0:T(8,128)(2,1)S(1)} dynamic-update-slice(bf16[2,16,24576]{2,1,0:T(8,128)(2,1)S(1)} %dynamic_update_slice.62, bf16[2,1,24576]{2,1,0:T(2,128)(2,1)S(1)} %copy.51, s32[]{:T(128)} %constant.115.clone.1, s32[]{:T(128)S(6)} %select_n.141, s32[]{:T(128)} %constant.115.clone.1) | dynamic-update-slice | bytes 196612 | tf_op jit(solution)/shard_map/dynamic_update_slice | solution.py:30
  236.0 1.1 copy-done.1
  (25 shorter events, 0.1 us)
Async XLA Ops:
  0.6 43.7 %copy-start = (bf16[1,2,16,24576]{3,2,1,0:T(8,128)(2,1)S(1)}, bf16[1,2,16,24576]{3,2,1,0:T(8,128)(2,1)}, u32[]{:S(2)}) copy-start(bf16[1,2,16,24576]{3,2,1,0:T(8,128)(2,1)} %param.4) | copy-start | bytes 4718596
  87.5 1.4 copy-start.5
  87.5 1.6 copy-start.3
  87.5 1.6 copy-start.4
  89.0 90.6 %copy-start.2 = (bf16[2,1,24576]{2,0,1:T(2,128)(2,1)}, bf16[2,1,24576]{2,0,1:T(2,128)(2,1)S(1)}, u32[]{:S(2)}) copy-start(bf16[2,1,24576]{2,0,1:T(2,128)(2,1)S(1)} %fusion.2) | copy-start | bytes 294916
  130.1 6.9 %collective-permute-start = (bf16[2,1,24576]{2,0,1:T(2,128)(2,1)S(1)}, bf16[2,1,24576]{2,0,1:T(2,128)(2,1)S(1)}, u32[]{:S(2)}, u32[]{:S(2)}) collective-permute-start(bf16[2,1,24576]{2,0,1:T(2,128)(2,1)S(1)} %divide_convert_fusion.1), channel_id=1, source_target_pairs={{0,2},{2,4},{4,6},{6,8},{8,10},{10,12},{12,14},{14,16},{16,18},{18... | collective-permute-start | bytes 294920 | tf_op jit(solution)/shard_map/ppermute | solution.py:29
  130.2 6.8 %collective-permute-start.1 = (bf16[2,1,24576]{2,0,1:T(2,128)(2,1)S(1)}, bf16[2,1,24576]{2,0,1:T(2,128)(2,1)S(1)}, u32[]{:S(2)}, u32[]{:S(2)}) collective-permute-start(bf16[2,1,24576]{2,0,1:T(2,128)(2,1)S(1)} %divide_convert_fusion.1), channel_id=1, source_target_pairs={{0,30},{2,0},{4,2},{6,4},{8,6},{10,8},{12,10},{14,12},{16,14},{18,... | collective-permute-start | bytes 294920 | tf_op jit(solution)/shard_map/ppermute | solution.py:34
  137.0 6.7 %collective-permute-start.2 = (bf16[2,1,24576]{2,0,1:T(2,128)(2,1)S(1)}, bf16[2,1,24576]{2,0,1:T(2,128)(2,1)S(1)}, u32[]{:S(2)}, u32[]{:S(2)}) collective-permute-start(bf16[2,1,24576]{2,0,1:T(2,128)(2,1)S(1)} %collective-permute-done), channel_id=1, source_target_pairs={{0,2},{2,4},{4,6},{6,8},{8,10},{10,12},{12,14},{14,16},{16,18},{18... | collective-permute-start | bytes 294920 | tf_op jit(solution)/shard_map/ppermute | solution.py:29
  137.0 6.7 %collective-permute-start.3 = (bf16[2,1,24576]{2,0,1:T(2,128)(2,1)S(1)}, bf16[2,1,24576]{2,0,1:T(2,128)(2,1)S(1)}, u32[]{:S(2)}, u32[]{:S(2)}) collective-permute-start(bf16[2,1,24576]{2,0,1:T(2,128)(2,1)S(1)} %collective-permute-done.1), channel_id=1, source_target_pairs={{0,30},{2,0},{4,2},{6,4},{8,6},{10,8},{12,10},{14,12},{16,14},{18,... | collective-permute-start | bytes 294920 | tf_op jit(solution)/shard_map/ppermute | solution.py:34
  143.8 6.7 %collective-permute-start.4 = (bf16[2,1,24576]{2,0,1:T(2,128)(2,1)S(1)}, bf16[2,1,24576]{2,0,1:T(2,128)(2,1)S(1)}, u32[]{:S(2)}, u32[]{:S(2)}) collective-permute-start(bf16[2,1,24576]{2,0,1:T(2,128)(2,1)S(1)} %collective-permute-done.2), channel_id=1, source_target_pairs={{0,2},{2,4},{4,6},{6,8},{8,10},{10,12},{12,14},{14,16},{16,18},{18... | collective-permute-start | bytes 294920 | tf_op jit(solution)/shard_map/ppermute | solution.py:29
  143.8 6.7 %collective-permute-start.5 = (bf16[2,1,24576]{2,0,1:T(2,128)(2,1)S(1)}, bf16[2,1,24576]{2,0,1:T(2,128)(2,1)S(1)}, u32[]{:S(2)}, u32[]{:S(2)}) collective-permute-start(bf16[2,1,24576]{2,0,1:T(2,128)(2,1)S(1)} %collective-permute-done.3), channel_id=1, source_target_pairs={{0,30},{2,0},{4,2},{6,4},{8,6},{10,8},{12,10},{14,12},{16,14},{18,... | collective-permute-start | bytes 294920 | tf_op jit(solution)/shard_map/ppermute | solution.py:34
  150.5 6.8 %collective-permute-start.6 = (bf16[2,1,24576]{2,0,1:T(2,128)(2,1)S(1)}, bf16[2,1,24576]{2,0,1:T(2,128)(2,1)S(1)}, u32[]{:S(2)}, u32[]{:S(2)}) collective-permute-start(bf16[2,1,24576]{2,0,1:T(2,128)(2,1)S(1)} %collective-permute-done.4), channel_id=1, source_target_pairs={{0,2},{2,4},{4,6},{6,8},{8,10},{10,12},{12,14},{14,16},{16,18},{18... | collective-permute-start | bytes 294920 | tf_op jit(solution)/shard_map/ppermute | solution.py:29
  150.5 6.8 %collective-permute-start.7 = (bf16[2,1,24576]{2,0,1:T(2,128)(2,1)S(1)}, bf16[2,1,24576]{2,0,1:T(2,128)(2,1)S(1)}, u32[]{:S(2)}, u32[]{:S(2)}) collective-permute-start(bf16[2,1,24576]{2,0,1:T(2,128)(2,1)S(1)} %collective-permute-done.5), channel_id=1, source_target_pairs={{0,30},{2,0},{4,2},{6,4},{8,6},{10,8},{12,10},{14,12},{16,14},{18,... | collective-permute-start | bytes 294920 | tf_op jit(solution)/shard_map/ppermute | solution.py:34
  157.4 6.7 %collective-permute-start.8 = (bf16[2,1,24576]{2,0,1:T(2,128)(2,1)S(1)}, bf16[2,1,24576]{2,0,1:T(2,128)(2,1)S(1)}, u32[]{:S(2)}, u32[]{:S(2)}) collective-permute-start(bf16[2,1,24576]{2,0,1:T(2,128)(2,1)S(1)} %collective-permute-done.6), channel_id=1, source_target_pairs={{0,2},{2,4},{4,6},{6,8},{8,10},{10,12},{12,14},{14,16},{16,18},{18... | collective-permute-start | bytes 294920 | tf_op jit(solution)/shard_map/ppermute | solution.py:29
  157.4 6.8 %collective-permute-start.9 = (bf16[2,1,24576]{2,0,1:T(2,128)(2,1)S(1)}, bf16[2,1,24576]{2,0,1:T(2,128)(2,1)S(1)}, u32[]{:S(2)}, u32[]{:S(2)}) collective-permute-start(bf16[2,1,24576]{2,0,1:T(2,128)(2,1)S(1)} %collective-permute-done.7), channel_id=1, source_target_pairs={{0,30},{2,0},{4,2},{6,4},{8,6},{10,8},{12,10},{14,12},{16,14},{18,... | collective-permute-start | bytes 294920 | tf_op jit(solution)/shard_map/ppermute | solution.py:34
  164.1 6.7 %collective-permute-start.10 = (bf16[2,1,24576]{2,0,1:T(2,128)(2,1)S(1)}, bf16[2,1,24576]{2,0,1:T(2,128)(2,1)S(1)}, u32[]{:S(2)}, u32[]{:S(2)}) collective-permute-start(bf16[2,1,24576]{2,0,1:T(2,128)(2,1)S(1)} %collective-permute-done.8), channel_id=1, source_target_pairs={{0,2},{2,4},{4,6},{6,8},{8,10},{10,12},{12,14},{14,16},{16,18},{18... | collective-permute-start | bytes 294920 | tf_op jit(solution)/shard_map/ppermute | solution.py:29
  164.1 6.8 %collective-permute-start.11 = (bf16[2,1,24576]{2,0,1:T(2,128)(2,1)S(1)}, bf16[2,1,24576]{2,0,1:T(2,128)(2,1)S(1)}, u32[]{:S(2)}, u32[]{:S(2)}) collective-permute-start(bf16[2,1,24576]{2,0,1:T(2,128)(2,1)S(1)} %collective-permute-done.9), channel_id=1, source_target_pairs={{0,30},{2,0},{4,2},{6,4},{8,6},{10,8},{12,10},{14,12},{16,14},{18,... | collective-permute-start | bytes 294920 | tf_op jit(solution)/shard_map/ppermute | solution.py:34
  170.8 6.7 %collective-permute-start.12 = (bf16[2,1,24576]{2,0,1:T(2,128)(2,1)S(1)}, bf16[2,1,24576]{2,0,1:T(2,128)(2,1)S(1)}, u32[]{:S(2)}, u32[]{:S(2)}) collective-permute-start(bf16[2,1,24576]{2,0,1:T(2,128)(2,1)S(1)} %collective-permute-done.10), channel_id=1, source_target_pairs={{0,2},{2,4},{4,6},{6,8},{8,10},{10,12},{12,14},{14,16},{16,18},{18... | collective-permute-start | bytes 294920 | tf_op jit(solution)/shard_map/ppermute | solution.py:29
  171.0 57.9 %collective-permute-start.13 = (bf16[2,1,24576]{2,0,1:T(2,128)(2,1)S(1)}, bf16[2,1,24576]{2,0,1:T(2,128)(2,1)S(1)}, u32[]{:S(2)}, u32[]{:S(2)}) collective-permute-start(bf16[2,1,24576]{2,0,1:T(2,128)(2,1)S(1)} %collective-permute-done.11), channel_id=1, source_target_pairs={{0,30},{2,0},{4,2},{6,4},{8,6},{10,8},{12,10},{14,12},{16,14},{18,... | collective-permute-start | bytes 294920 | tf_op jit(solution)/shard_map/ppermute | solution.py:34
  177.6 54.8 %collective-permute-start.14 = (bf16[2,1,24576]{2,0,1:T(2,128)(2,1)S(1)}, bf16[2,1,24576]{2,0,1:T(2,128)(2,1)S(1)}, u32[]{:S(2)}, u32[]{:S(2)}) collective-permute-start(bf16[2,1,24576]{2,0,1:T(2,128)(2,1)S(1)} %collective-permute-done.12), channel_id=1, source_target_pairs={{0,2},{2,4},{4,6},{6,8},{8,10},{10,12},{12,14},{14,16},{16,18},{18... | collective-permute-start | bytes 294920 | tf_op jit(solution)/shard_map/ppermute | solution.py:29
  236.0 1.1 copy-start.1
